TPU v7x, 16 devices: a 4x2x1 block of a 4x4x8 slice. The times are simulated.
16 devices in a mesh: pod: 2 (over y, z), mp: 8 (over x, core).
Axes of the slice: x: 4, y: 2, z: 1, core: 2. Of those that a mesh axis runs over, the one named last changes fastest.
The devices are a block of a 4x4x8 slice.
Arguments:
- d_pool: bfloat16 [32768, 26, 128], P(('pod', 'mp')), parts along dimension 0
- row_ids: int32 [64, 16384, 1], P(('pod', 'mp')), parts along dimension 0
- lengths: int32 [64, 16384], P(('pod', 'mp')), parts along dimension 0
- tables: bfloat16 [64, 16384, 128], P(('pod', 'mp')), parts along dimension 0
- row_accum: float32 [64, 16384], P(('pod', 'mp')), parts along dimension 0
- learn_rate: float32 [], replicated
Outputs:
- output 1: bfloat16 [64, 16384, 128], P(('pod', 'mp')), parts along dimension 0
- output 2: float32 [64, 16384], P(('pod', 'mp')), parts along dimension 0
There are 2 independent parts. A program takes and returns all parts, laid end to end along the dimension named above; an argument that names none is the same for every part.
All inputs are finite; a program needn't handle non-finite values.
Results may differ from a plain program's by a relative error of at most 0.001.
Values are sent between devices in bfloat16 or wider.
A program may use at most 768 MiB of HBM per device.

v0:
```python
import jax
import jax.numpy as jnp
from jax import lax
from jax.sharding import PartitionSpec as P

EPSILON = 1e-06


def scatter_rows(owned_grad, row_ids, lengths, n_rows):
    slots_dev, batch_all, emb_dim = owned_grad.shape
    grad_vals = owned_grad.astype(jnp.float32).reshape(slots_dev * batch_all, emb_dim)
    row_offset = (jnp.arange(slots_dev, dtype=jnp.int32) * n_rows)[:, None]
    dropped = slots_dev * n_rows

    def add_position(pos_idx, row_grad):
        pos_ids = lax.dynamic_index_in_dim(row_ids, pos_idx, axis=2, keepdims=False)
        seg_rows = jnp.where(pos_idx < lengths, pos_ids + row_offset, dropped).reshape(-1)
        return row_grad.at[seg_rows].add(grad_vals, mode='drop')

    row_grad = lax.fori_loop(0, row_ids.shape[2], add_position, jnp.zeros((dropped, emb_dim), jnp.float32))
    return row_grad.reshape(slots_dev, n_rows, emb_dim)


def adagrad_rows(tables, row_accum, row_grad, learn_rate):
    new_accum = row_accum + jnp.mean(row_grad * row_grad, axis=-1)
    row_scale = learn_rate / (jnp.sqrt(new_accum) + EPSILON)
    new_tables = (tables.astype(jnp.float32) - row_grad * row_scale[..., None]).astype(jnp.bfloat16)
    return new_tables, new_accum


def solution(mesh):
    n_group = mesh.shape['mp']
    slot_spec = P(('pod', 'mp'))

    def local_step(d_pool, row_ids, lengths, tables, row_accum, learn_rate):
        n_tab = d_pool.shape[1]
        slots_dev = tables.shape[0]
        padded = jnp.pad(d_pool, ((0, 0), (0, slots_dev * n_group - n_tab), (0, 0)))
        owned_all = lax.all_to_all(padded, 'mp', 1, 0, tiled=True)
        owned_grad = jnp.swapaxes(owned_all, 0, 1)
        row_grad = scatter_rows(owned_grad, row_ids, lengths, tables.shape[1])
        return adagrad_rows(tables, row_accum, row_grad, learn_rate)

    return jax.shard_map(local_step, mesh=mesh, in_specs=(slot_spec, slot_spec, slot_spec, slot_spec, slot_spec, P()), out_specs=(slot_spec, slot_spec), check_vma=False)
```

profile of v0, /device:TPU:112, one launch (start us, length us, event | category | flops | bytes accessed | tf_op | source)
XLA Modules:
  0.0 624.0 jit_solution(6210294437270206450)
XLA Ops:
  0.6 0.0 copy-start
  0.6 0.0 copy-start.1
  0.6 13.9 %pad.4 = bf16[2048,32,128]{2,0,1:T(8,128)(2,1)} pad(bf16[2048,26,128]{2,0,1:T(8,128)(2,1)} %param.6, bf16[]{:T(256)} %constant.18.clone.1), padding=0_0x0_6x0_0 | pad | bytes 30408706 | tf_op jit(solution)/shard_map/jit(_pad)/pad | solution.py:38
  14.5 5.9 all-to-all-start
  20.5 0.0 copy-done
  20.5 0.0 copy-done.1
  20.5 0.2 fusion.3
  20.7 0.3 copy.10
  21.6 0.3 compare_select_fusion
  21.9 183.0 %all-to-all-done = bf16[2048,32,128]{2,0,1:T(8,128)(2,1)} async-done(((bf16[2048,32,128]{2,0,1:T(8,128)(2,1)}), bf16[2048,32,128]{2,0,1:T(8,128)(2,1)}, u32[]{:S(2)}, u32[]{:S(2)}) %all-to-all-start) | async-done | bytes 16777248 | tf_op jit(solution)/shard_map/all_to_all | solution.py:39
  204.9 8.5 %convert_bitcast_fusion = f32[8,2048,4,128]{3,1,2,0:T(8,128)S(1)} fusion(bf16[2048,8,4,128]{3,0,2,1:T(8,128)(2,1)} %bitcast.7), kind=kLoop, calls=%fused_computation.1 | loop fusion | flops 8388608 | bytes 50331648 | tf_op jit(solution)/shard_map/reshape | solution.py:11
  213.5 11.0 %copy.8 = f32[8,2048,4,128]{3,1,0,2:T(8,128)} copy(f32[8,2048,4,128]{3,1,2,0:T(8,128)S(1)} %convert_bitcast_fusion) | data formatting | bytes 67108864 | tf_op jit(solution)/shard_map/reshape | solution.py:11
  224.5 0.0 copy-start.2
  224.5 360.6 %scatter_custom_fusion = f32[65536,128]{1,0:T(8,128)} fusion(s32[65536]{0:T(1024)S(1)} %bitcast.25, f32[65536,128]{1,0:T(8,128)} %bitcast.23, f32[]{:T(128)} %constant.8.clone.1), kind=kCustom, calls=%fused_computation.4 | custom fusion | flops 8388608 | bytes 33554944 | tf_op jit(solution)/shard_map/while/body/eval_jaxpr/scatter-add | solution.py:18
  585.1 15.3 %multiply_reduce_fusion = f32[65536]{0:T(1024)S(1)} fusion(f32[65536,128]{1,0:T(8,128)} %scatter_custom_fusion), kind=kLoop, calls=%fused_computation.3 | loop fusion | flops 16711680 | bytes 33816576 | tf_op jit(solution)/shard_map/reduce_sum | solution.py:25
  600.4 0.1 div.17
  600.5 0.0 copy-done.2
  600.5 0.9 add_divide_fusion
  601.4 22.6 %subtract_convert_fusion = bf16[4,16384,128]{2,1,0:T(8,128)(2,1)} fusion(f32[4,16384,128]{2,1,0:T(8,128)} %bitcast.22, bf16[4,16384,128]{2,1,0:T(8,128)(2,1)} %param.9, f32[4,16384]{1,0:T(4,128)S(1)} %get-tuple-element.16), kind=kLoop, calls=%fused_computation.2 | loop fusion | flops 33554432 | bytes 67371008 | tf_op jit(solution)/shard_map/convert_element_type | solution.py:27
  (2 shorter events, 0.0 us)
Async XLA Ops:
  0.6 19.8 %copy-start = (s32[4,16384,1]{1,2,0:T(1,128)S(1)}, s32[4,16384,1]{1,2,0:T(1,128)}, u32[]{:S(2)}) copy-start(s32[4,16384,1]{1,2,0:T(1,128)} %param.7) | copy-start | bytes 786436
  0.6 19.8 %copy-start.1 = (s32[4,16384]{1,0:T(4,128)S(1)}, s32[4,16384]{1,0:T(4,128)}, u32[]{:S(2)}) copy-start(s32[4,16384]{1,0:T(4,128)} %param.8) | copy-start | bytes 786436
  14.5 190.4 %all-to-all-start = ((bf16[2048,32,128]{2,0,1:T(8,128)(2,1)}), bf16[2048,32,128]{2,0,1:T(8,128)(2,1)}, u32[]{:S(2)}, u32[]{:S(2)}) async-start(bf16[2048,32,128]{2,0,1:T(8,128)(2,1)} %pad.4), calls=%async_computation | async-start | bytes 33554432 | tf_op jit(solution)/shard_map/all_to_all | solution.py:39
  224.5 376.1 %copy-start.2 = (f32[4,16384]{1,0:T(4,128)S(1)}, f32[4,16384]{1,0:T(4,128)}, u32[]{:S(2)}) copy-start(f32[4,16384]{1,0:T(4,128)} %param.10) | copy-start | bytes 786436
where the time goes:
time: 625 us; the launch traced here: 624 us
  other arithmetic  408 us (65%)
  waiting for transfers between devices  183 us (29%)
  local copies, waits for them, and re-layouts  25.3 us (4%)
    scatter-add x1, other arithmetic, add_position(): return row_grad.at[seg_rows].add(grad_vals, mode='drop')  361 us
    all_to_all x1, waiting for transfers between devices, local_step(): owned_all = lax.all_to_all(padded, 'mp', 1, 0, tiled=True)  183 us
    convert_element_type x1, other arithmetic, adagrad_rows(): (tables.astype(jnp.float32) - row_grad * row_scale[..., None]).astype(jnp...  22.6 us
    reduce_sum x1, other arithmetic, adagrad_rows(): new_accum = row_accum + jnp.mean(row_grad * row_grad, axis=-1)  15.3 us
    pad x1, local copies, waits for them, and re-layouts, local_step(): padded = jnp.pad(d_pool, ((0, 0), (0, slots_dev * n_group - n_tab), (0, 0)))  13.9 us
  transfers between devices with their start and end apart: 1, of which 1 were waited for; matrix products, arithmetic and copies ran while one was open for 0% of the time, Pallas kernels for 0%

commit v1 on v0

v1 whole, which is shorter than its diff:
```python
import jax
import jax.numpy as jnp
from jax import lax
from jax.experimental import pallas as pl
from jax.experimental.pallas import tpu as pltpu
from jax.sharding import PartitionSpec as P


EPSILON = 1e-06
LANES = 128
N_ACC = 4
UNROLL = 16


def scatter_adagrad_kernel(ids_ref, lr_ref, grad_ref, table_ref, accum_ref, *refs):
    new_table_ref, new_accum_ref, grad_f32, *accs = refs[-(N_ACC + 3):]
    step = pl.program_id(0)
    n_blk = grad_f32.shape[0]
    n_rows = table_ref.shape[0]

    @pl.when(step == 0)
    def _():
        def zero(i, carry):
            for acc in accs:
                acc[pl.ds(pl.multiple_of(i * 64, 64), 64), :] = jnp.zeros((64, LANES), jnp.float32)
            return carry

        lax.fori_loop(0, n_rows // 64, zero, 0)

    def widen(i, carry):
        rows = pl.ds(pl.multiple_of(i * 128, 128), 128)
        grad_f32[rows, :] = grad_ref[rows, :].astype(jnp.float32)
        return carry

    lax.fori_loop(0, n_blk // 128, widen, 0)

    def add_rows(i, carry):
        base = i * UNROLL
        for first in range(0, UNROLL, N_ACC):
            rows = [ids_ref[step * n_blk + base + first + k] for k in range(N_ACC)]
            sums = [accs[k][pl.ds(rows[k], 1), :] + grad_f32[pl.ds(base + first + k, 1), :] for k in range(N_ACC)]
            for k in range(N_ACC):
                accs[k][pl.ds(rows[k], 1), :] = sums[k]
        return carry

    lax.fori_loop(0, n_blk // UNROLL, add_rows, 0)

    @pl.when(step == pl.num_programs(0) - 1)
    def _():
        lr = lr_ref[0]
        diag = lax.broadcasted_iota(jnp.int32, (LANES, LANES), 0) == lax.broadcasted_iota(jnp.int32, (LANES, LANES), 1)

        def update(i, carry):
            rows = pl.ds(pl.multiple_of(i * LANES, LANES), LANES)
            grad = accs[0][rows, :]
            for acc in accs[1:]:
                grad = grad + acc[rows, :]
            old = jnp.broadcast_to(accum_ref[pl.ds(i, 1), :], (LANES, LANES))
            col = jnp.sum(grad * grad * (1.0 / LANES) + jnp.where(diag, old, 0.0), axis=1, keepdims=True)
            scale = lr / (jnp.sqrt(col) + EPSILON)
            new_table_ref[rows, :] = (table_ref[rows, :].astype(jnp.float32) - grad * scale).astype(jnp.bfloat16)
            new_accum_ref[pl.ds(i, 1), :] = jnp.sum(jnp.where(diag, col, 0.0), axis=0, keepdims=True)
            return carry

        lax.fori_loop(0, n_rows // LANES, update, 0)


def scatter_adagrad(slot, ids, learn_rate, grads, tables, accum, prev):
    n_src, n_blk, dim = grads.shape
    _, n_rows, _ = tables.shape
    once = pl.Buffered(1)
    grid_spec = pltpu.PrefetchScalarGridSpec(
        num_scalar_prefetch=2,
        grid=(n_src,),
        in_specs=[
            pl.BlockSpec((None, n_blk, dim), lambda s, *_: (s, 0, 0)),
            pl.BlockSpec((None, n_rows, dim), lambda s, *_: (slot, 0, 0), pipeline_mode=once),
            pl.BlockSpec((None, n_rows // LANES, LANES), lambda s, *_: (slot, 0, 0), pipeline_mode=once),
        ]
        + [pl.BlockSpec(memory_space=pl.ANY) for _ in prev],
        out_specs=[
            pl.BlockSpec((None, n_rows, dim), lambda s, *_: (slot, 0, 0), pipeline_mode=once),
            pl.BlockSpec((None, n_rows // LANES, LANES), lambda s, *_: (slot, 0, 0), pipeline_mode=once),
        ],
        scratch_shapes=[pltpu.VMEM((n_blk, dim), jnp.float32)]
        + [pltpu.VMEM((n_rows + 8, dim), jnp.float32) for _ in range(N_ACC)],
    )
    return pl.pallas_call(
        scatter_adagrad_kernel,
        grid_spec=grid_spec,
        out_shape=[jax.ShapeDtypeStruct(tables.shape, tables.dtype), jax.ShapeDtypeStruct(accum.shape, accum.dtype)],
        input_output_aliases={5: 0, 6: 1} if prev else {},
        compiler_params=pltpu.CompilerParams(vmem_limit_bytes=60 * 1024 * 1024),
        cost_estimate=pl.CostEstimate(flops=4_000_000_000, bytes_accessed=16 * 1024 * 1024, transcendentals=0),
        name="scatter_adagrad",
    )(ids, learn_rate, grads, tables, accum, *prev)


def solution(mesh):
    n_group = mesh.shape['mp']
    slot_spec = P(('pod', 'mp'))

    def local_step(d_pool, row_ids, lengths, tables, row_accum, learn_rate):
        n_tab = d_pool.shape[1]
        slots_dev, n_rows, dim = tables.shape
        by_slot = jnp.swapaxes(d_pool, 0, 1)
        padded = jnp.pad(by_slot, ((0, slots_dev * n_group - n_tab), (0, 0), (0, 0)))
        by_owner = padded.reshape(n_group, slots_dev, d_pool.shape[0], dim)
        ids = jnp.where(lengths > 0, row_ids[:, :, 0], n_rows)
        accum = row_accum.reshape(slots_dev, n_rows // LANES, LANES)
        lr = learn_rate.reshape(1)
        recv = []
        for j in range(slots_dev):
            send = by_owner[:, j]
            if recv:
                send, recv[-1] = lax.optimization_barrier((send, recv[-1]))
            recv.append(lax.all_to_all(send, 'mp', 0, 0, tiled=True))
        out = ()
        for j in range(slots_dev):
            out = scatter_adagrad(j, ids[j], lr, recv[j], tables, accum, out)
        return out[0], out[1].reshape(slots_dev, n_rows)

    return jax.shard_map(local_step, mesh=mesh, in_specs=(slot_spec, slot_spec, slot_spec, slot_spec, slot_spec, P()), out_specs=(slot_spec, slot_spec), check_vma=False)
```

time: 625 us -> 406 us (0.65)
  the two profiles are of different devices: /device:TPU:112 before, /device:TPU:119 now
where the time goes in v1:
time: 406 us; the launch traced here: 405 us
  Pallas kernels  221 us (54%)
  blocking collectives  105 us (26%)
  waiting for transfers between devices  45.4 us (11%)
  local copies, waits for them, and re-layouts  17.5 us (4%)
  starting transfers between devices  14.7 us (4%)
    pallas_call x4, Pallas kernels, scatter_adagrad(): pl.pallas_call(scatter_adagrad_kernel, grid_spec=grid_spec, out_shape=[ja...  221 us
    all_to_all x2, blocking collectives, local_step(): recv.append(lax.all_to_all(send, 'mp', 0, 0, tiled=True))  105 us
    all_to_all x2, waiting for transfers between devices, local_step(): recv.append(lax.all_to_all(send, 'mp', 0, 0, tiled=True))  45.4 us
    all_to_all x2, starting transfers between devices, local_step(): recv.append(lax.all_to_all(send, 'mp', 0, 0, tiled=True))  14.7 us
  transfers between devices with their start and end apart: 2, of which 1 were waited for; matrix products, arithmetic and copies ran while one was open for 0% of the time, Pallas kernels for 41%

profile of v1, /device:TPU:119, one launch (start us, length us, event | category | flops | bytes accessed | tf_op | source)
XLA Modules:
  0.0 405.2 jit_solution(5153184847092972303)
XLA Ops:
  0.6 8.0 %pad.4 = bf16[32,2048,128]{2,1,0:T(8,128)(2,1)S(1)} pad(bf16[26,2048,128]{2,1,0:T(8,128)(2,1)} %bitcast.38, bf16[]{:T(256)} %constant.6.clone.1), padding=0_6x0_0x0_0 | pad | bytes 30408706 | tf_op jit(solution)/shard_map/jit(_pad)/pad | solution.py:107
  8.7 6.0 %slice_bitcast_fusion = (bf16[8,2048,128]{2,1,0:T(8,128)(2,1)}, bf16[8,2048,128]{2,1,0:T(8,128)(2,1)}, bf16[8,2048,128]{2,1,0:T(8,128)(2,1)}, bf16[8,2048,128]{2,1,0:T(8,128)(2,1)}) fusion(bf16[8,4,2048,128]{3,2,1,0:T(8,128)(2,1)S(1)} %bitcast.37), kind=kLoop, calls=%fused_computation | loop fusion | bytes 33554432 | tf_op jit(solution)/shard_map/squeeze | solution.py:114
  14.7 0.0 copy-start
  14.7 52.2 %all_to_all.20.grad_ref = bf16[8,2048,128]{2,1,0:T(8,128)(2,1)} all-to-all(bf16[8,2048,128]{2,1,0:T(8,128)(2,1)} %get-tuple-element.30), channel_id=1, replica_groups=mesh['pod'=2,'mp'=8] {'mp'}, dimensions={0} | all-to-all | bytes 8388608 | tf_op jit(solution)/shard_map/all_to_all | solution.py:117
  66.9 0.0 copy-done
  66.9 53.0 %all_to_all.21.grad_ref = bf16[8,2048,128]{2,1,0:T(8,128)(2,1)} all-to-all(bf16[8,2048,128]{2,1,0:T(8,128)(2,1)S(1)} %copy-done), channel_id=1, replica_groups=mesh['pod'=2,'mp'=8] {'mp'}, dimensions={0} | all-to-all | bytes 8388608 | tf_op jit(solution)/shard_map/all_to_all | solution.py:117
  119.9 0.0 copy-start.3
  119.9 0.0 copy-start.1
  119.9 0.0 copy-start.2
  119.9 7.5 %all-to-all-start.2 = ((bf16[8,2048,128]{2,1,0:T(8,128)(2,1)}), bf16[8,2048,128]{2,1,0:T(8,128)(2,1)}, u32[]{:S(2)}, u32[]{:S(2)}) async-start(bf16[8,2048,128]{2,1,0:T(8,128)(2,1)} %get-tuple-element.17), calls=%async_computation.2 | async-start | bytes 8388608 | tf_op jit(solution)/shard_map/all_to_all | solution.py:117
  128.0 0.0 copy-done.3
  128.0 0.7 copy.29
  128.7 0.0 copy-done.1
  128.7 0.0 copy-done.2
  128.7 0.2 bitcast_select_fusion
  129.0 45.4 %all-to-all-done.2.grad_ref = bf16[8,2048,128]{2,1,0:T(8,128)(2,1)} async-done(((bf16[8,2048,128]{2,1,0:T(8,128)(2,1)}), bf16[8,2048,128]{2,1,0:T(8,128)(2,1)}, u32[]{:S(2)}, u32[]{:S(2)}) %all-to-all-start.2) | async-done | bytes 4194336 | tf_op jit(solution)/shard_map/all_to_all | solution.py:117
  174.4 7.2 %all-to-all-start.3 = ((bf16[8,2048,128]{2,1,0:T(8,128)(2,1)}), bf16[8,2048,128]{2,1,0:T(8,128)(2,1)}, u32[]{:S(2)}, u32[]{:S(2)}) async-start(bf16[8,2048,128]{2,1,0:T(8,128)(2,1)} %get-tuple-element.18), calls=%async_computation.3 | async-start | bytes 8388608 | tf_op jit(solution)/shard_map/all_to_all | solution.py:117
  181.6 0.9 fusion
  182.5 55.2 %scatter_adagrad.4 = (bf16[4,16384,128]{2,1,0:T(8,128)(2,1)}, f32[4,128,128]{2,1,0:T(8,128)}) custom-call(s32[16384]{0:T(1024)} %bitcast.47, f32[1]{0:T(128)} %bitcast.33.lr_ref, bf16[8,2048,128]{2,1,0:T(8,128)(2,1)} %all_to_all.20.grad_ref, bf16[4,16384,128]{2,1,0:T(8,128)(2,1)} %table_ref.7, f32[4,128,128]{2,1,0:T(8,128)} %bitcast.39), custom_call_target="tpu_custom_call" | custom-call | flops 4000000000 | bytes 16777216 | tf_op jit(solution)/shard_map/scatter_adagrad/pallas_call | solution.py:88
  237.7 55.2 %scatter_adagrad.5 = (bf16[4,16384,128]{2,1,0:T(8,128)(2,1)}, f32[4,128,128]{2,1,0:T(8,128)}) custom-call(s32[16384]{0:T(1024)} %bitcast.46, f32[1]{0:T(128)} %bitcast.34.lr_ref, bf16[8,2048,128]{2,1,0:T(8,128)(2,1)} %all_to_all.21.grad_ref, bf16[4,16384,128]{2,1,0:T(8,128)(2,1)} %table_ref.7, ...), custom_call_target="tpu_custom_call", output_to_operand_aliasing={{0}: (5, {}), {1}: (6, {})} | custom-call | flops 4000000000 | bytes 16777216 | tf_op jit(solution)/shard_map/scatter_adagrad/pallas_call | solution.py:88
  292.9 55.2 %scatter_adagrad.6 = (bf16[4,16384,128]{2,1,0:T(8,128)(2,1)}, f32[4,128,128]{2,1,0:T(8,128)}) custom-call(s32[16384]{0:T(1024)} %bitcast.45, f32[1]{0:T(128)} %bitcast.35.lr_ref, bf16[8,2048,128]{2,1,0:T(8,128)(2,1)} %all-to-all-done.2.grad_ref, bf16[4,16384,128]{2,1,0:T(8,128)(2,1)} %table_ref.7, ...), custom_call_target="tpu_custom_call", output_to_operand_aliasing={{0}: (5, {}), {1}: (6, {})} | custom-call | flops 4000000000 | bytes 16777216 | tf_op jit(solution)/shard_map/scatter_adagrad/pallas_call | solution.py:88
  348.2 0.0 all-to-all-done.3.grad_ref
  348.2 55.2 %scatter_adagrad.7 = (bf16[4,16384,128]{2,1,0:T(8,128)(2,1)}, f32[4,128,128]{2,1,0:T(8,128)}) custom-call(s32[16384]{0:T(1024)} %bitcast.44, f32[1]{0:T(128)} %bitcast.36.lr_ref, bf16[8,2048,128]{2,1,0:T(8,128)(2,1)} %all-to-all-done.3.grad_ref, bf16[4,16384,128]{2,1,0:T(8,128)(2,1)} %table_ref.7, ...), custom_call_target="tpu_custom_call", output_to_operand_aliasing={{0}: (5, {}), {1}: (6, {})} | custom-call | flops 4000000000 | bytes 16777216 | tf_op jit(solution)/shard_map/scatter_adagrad/pallas_call | solution.py:88
  403.4 1.8 copy.28
Async XLA Ops:
  14.7 52.2 %copy-start = (bf16[8,2048,128]{2,1,0:T(8,128)(2,1)S(1)}, bf16[8,2048,128]{2,1,0:T(8,128)(2,1)}, u32[]{:S(2)}) copy-start(bf16[8,2048,128]{2,1,0:T(8,128)(2,1)} %get-tuple-element.16) | copy-start | bytes 12582916
  119.9 8.1 %copy-start.3 = (f32[4,16384]{1,0:T(4,128)S(1)}, f32[4,16384]{1,0:T(4,128)}, u32[]{:S(2)}) copy-start(f32[4,16384]{1,0:T(4,128)} %param.10) | copy-start | bytes 786436
  119.9 8.9 %copy-start.1 = (s32[4,16384,1]{1,2,0:T(1,128)S(1)}, s32[4,16384,1]{1,2,0:T(1,128)}, u32[]{:S(2)}) copy-start(s32[4,16384,1]{1,2,0:T(1,128)} %param.7) | copy-start | bytes 786436
  119.9 8.9 %copy-start.2 = (s32[4,16384]{1,0:T(4,128)S(1)}, s32[4,16384]{1,0:T(4,128)}, u32[]{:S(2)}) copy-start(s32[4,16384]{1,0:T(4,128)} %param.8) | copy-start | bytes 786436
  119.9 54.5 %all-to-all-start.2 = ((bf16[8,2048,128]{2,1,0:T(8,128)(2,1)}), bf16[8,2048,128]{2,1,0:T(8,128)(2,1)}, u32[]{:S(2)}, u32[]{:S(2)}) async-start(bf16[8,2048,128]{2,1,0:T(8,128)(2,1)} %get-tuple-element.17), calls=%async_computation.2 | async-start | bytes 8388608 | tf_op jit(solution)/shard_map/all_to_all | solution.py:117
  174.4 173.8 %all-to-all-start.3 = ((bf16[8,2048,128]{2,1,0:T(8,128)(2,1)}), bf16[8,2048,128]{2,1,0:T(8,128)(2,1)}, u32[]{:S(2)}, u32[]{:S(2)}) async-start(bf16[8,2048,128]{2,1,0:T(8,128)(2,1)} %get-tuple-element.18), calls=%async_computation.3 | async-start | bytes 8388608 | tf_op jit(solution)/shard_map/all_to_all | solution.py:117

commit v2 on v1

v2 whole, which is shorter than its diff:
```python
import functools

import jax
import jax.numpy as jnp
from jax import lax
from jax.experimental import pallas as pl
from jax.experimental.pallas import tpu as pltpu
from jax.sharding import PartitionSpec as P


EPSILON = 1e-06
LANES = 128
N_ACC = 4
UNROLL = 16
SLOTS_PER_DEVICE = 4
FLAG_ROWS = 8
CAPACITY_SHARES = (9, 12, 16)
MIB = 1024 * 1024


def positions_kernel(lens_ref, out_ref):
    n_group, rows_out, _ = out_ref.shape
    per_group = rows_out - FLAG_ROWS
    n_rows = lens_ref.shape[0]
    slots_dev = n_group and n_rows // (n_group * (per_group // SLOTS_PER_DEVICE))
    blocks = per_group // slots_dev
    valid = (lens_ref[...] > 0).astype(jnp.bfloat16)
    lane_i = lax.broadcasted_iota(jnp.int32, (LANES, LANES), 0)
    lane_j = lax.broadcasted_iota(jnp.int32, (LANES, LANES), 1)
    before = (lane_i < lane_j).astype(jnp.bfloat16)
    inside = jnp.dot(valid, before, preferred_element_type=jnp.float32)
    total = jnp.dot(valid, jnp.ones((LANES, LANES), jnp.bfloat16), preferred_element_type=jnp.float32)
    row_i = lax.broadcasted_iota(jnp.int32, (n_rows, n_rows), 0)
    row_j = lax.broadcasted_iota(jnp.int32, (n_rows, n_rows), 1)
    earlier = ((row_j < row_i) & (row_j // blocks == row_i // blocks)).astype(jnp.bfloat16)
    ahead = jnp.dot(earlier, total.astype(jnp.bfloat16), preferred_element_type=jnp.float32)
    code = ((inside + ahead) * 2.0 + valid.astype(jnp.float32)).astype(jnp.int32)
    largest = jnp.max(ahead + total, axis=0, keepdims=True).astype(jnp.int32)
    for d in range(n_group):
        for j in range(slots_dev):
            first = (j * n_group + d) * blocks
            out_ref[d, j * blocks : (j + 1) * blocks, :] = code[first : first + blocks, :]
        out_ref[d, per_group:, :] = jnp.broadcast_to(largest, (FLAG_ROWS, LANES))


def bag_positions(lengths, n_group):
    slots_dev, batch_all = lengths.shape
    per_group = slots_dev * batch_all // (n_group * LANES)
    return pl.pallas_call(
        positions_kernel,
        out_shape=jax.ShapeDtypeStruct((n_group, per_group + FLAG_ROWS, LANES), jnp.int32),
        name="bag_positions",
    )(lengths.reshape(slots_dev * batch_all // LANES, LANES))


def pack_rows_kernel(slot, n_tab, slots_dev, first_ref, code_ref, grad_ref, out_ref, packed):
    dst = pl.program_id(0)
    blocks = grad_ref.shape[0] // LANES
    cap = out_ref.shape[0]

    @pl.when(dst * slots_dev + slot < n_tab)
    def _():
        code = code_ref[slot * blocks : (slot + 1) * blocks, :]
        pos = code >> 1
        rel = jnp.where((code & 1) == 1, pos - pos[:, :1], -1).astype(jnp.float32)
        target = lax.broadcasted_iota(jnp.int32, (LANES, LANES), 0).astype(jnp.float32)
        for b in range(blocks):
            pick = jnp.where(target == rel[b : b + 1, :], 1.0, 0.0).astype(jnp.bfloat16)
            rows = jnp.dot(pick, grad_ref[b * LANES : (b + 1) * LANES, :], preferred_element_type=jnp.float32)
            first = first_ref[(dst * slots_dev + slot) * blocks + b]
            packed[pl.ds(first, LANES), :] = rows

        def narrow(i, carry):
            rows = pl.ds(pl.multiple_of(i * LANES, LANES), LANES)
            out_ref[rows, :] = packed[rows, :].astype(jnp.bfloat16)
            return carry

        lax.fori_loop(0, cap // LANES, narrow, 0)


def pack_rows(slot, slots_dev, cap, firsts, codes, by_slot):
    n_tab, batch, dim = by_slot.shape
    n_group = codes.shape[0]
    grid_spec = pltpu.PrefetchScalarGridSpec(
        num_scalar_prefetch=1,
        grid=(n_group,),
        in_specs=[
            pl.BlockSpec((None,) + codes.shape[1:], lambda d, *_: (d, 0, 0)),
            pl.BlockSpec((None, batch, dim), lambda d, *_: (jnp.minimum(d * slots_dev + slot, n_tab - 1), 0, 0)),
        ],
        out_specs=pl.BlockSpec((None, cap, dim), lambda d, *_: (d, 0, 0)),
        scratch_shapes=[pltpu.VMEM((cap + LANES, dim), jnp.float32)],
    )
    return pl.pallas_call(
        functools.partial(pack_rows_kernel, slot, n_tab, slots_dev),
        grid_spec=grid_spec,
        out_shape=jax.ShapeDtypeStruct((n_group, cap, dim), by_slot.dtype),
        cost_estimate=pl.CostEstimate(flops=500_000_000, bytes_accessed=8 * MIB, transcendentals=0),
        name="pack_rows",
    )(firsts, codes, by_slot)


def pack_ids_kernel(first_ref, code_ref, ids_ref, out_ref, packed, *, n_rows):
    slot = pl.program_id(0)
    n_group = code_ref.shape[0]
    blocks = ids_ref.shape[0] // n_group
    per_src = out_ref.shape[0] // n_group
    slots_dev = pl.num_programs(0)
    n_high = n_rows // LANES
    target = lax.broadcasted_iota(jnp.int32, (2 * LANES, LANES), 0).astype(jnp.float32)
    part = lax.broadcasted_iota(jnp.int32, (8, LANES), 0)

    def one_source(src, carry):
        packed[...] = jnp.zeros_like(packed)
        for b in range(blocks):
            row = first_ref[(src * slots_dev + slot) * blocks + b] // LANES
            code = code_ref[src, pl.ds(slot * blocks + b, 1), :]
            rel = jnp.where((code & 1) == 1, (code >> 1) - row * LANES, -1).astype(jnp.float32)
            pick = jnp.where(target == rel, 1.0, 0.0).astype(jnp.bfloat16)
            ids = ids_ref[pl.ds(src * blocks + b, 1), :]
            parts = jnp.where(part == 0, n_high - ids // LANES, jnp.where(part == 1, ids % LANES, 0)).astype(jnp.bfloat16)
            moved = lax.dot_general(parts, pick, (((1,), (1,)), ((), ())), preferred_element_type=jnp.float32)
            packed[row] = packed[row] + moved[:, :LANES]
            packed[row + 1] = packed[row + 1] + moved[:, LANES:]
        for r in range(per_src):
            both = packed[r].astype(jnp.int32)
            out_ref[pl.ds(src * per_src + r, 1), :] = (n_high - both[0:1, :]) * LANES + both[1:2, :]
        return carry

    lax.fori_loop(0, n_group, one_source, 0)


def pack_ids(cap, firsts, codes, ids, n_rows):
    slots_dev, batch_all = ids.shape
    n_group = codes.shape[0]
    rows_out = n_group * cap // LANES
    grid_spec = pltpu.PrefetchScalarGridSpec(
        num_scalar_prefetch=1,
        grid=(slots_dev,),
        in_specs=[
            pl.BlockSpec(codes.shape, lambda j, *_: (0, 0, 0)),
            pl.BlockSpec((None, batch_all // LANES, LANES), lambda j, *_: (j, 0, 0)),
        ],
        out_specs=pl.BlockSpec((None, rows_out, LANES), lambda j, *_: (j, 0, 0)),
        scratch_shapes=[pltpu.VMEM((cap // LANES + 2, 8, LANES), jnp.float32)],
    )
    return pl.pallas_call(
        functools.partial(pack_ids_kernel, n_rows=n_rows),
        grid_spec=grid_spec,
        out_shape=jax.ShapeDtypeStruct((slots_dev, rows_out, LANES), jnp.int32),
        cost_estimate=pl.CostEstimate(flops=1_000_000_000, bytes_accessed=MIB, transcendentals=0),
        name="pack_ids",
    )(firsts, codes, ids.reshape(slots_dev, batch_all // LANES, LANES))


def scatter_adagrad_kernel(slot, n_prev, ids_ref, count_ref, lr_ref, grad_ref, table_hbm, accum_ref, *refs):
    prev_refs, refs = refs[:n_prev], refs[n_prev:]
    new_table_hbm, new_accum_ref, grad_f32, table, scale_ref, sems, *accs = refs
    step = pl.program_id(0)
    cap = grad_f32.shape[0]
    n_rows = table.shape[0]
    n_out = sems.shape[0] - 1
    load_table = pltpu.make_async_copy(table_hbm.at[slot], table, sems.at[n_out])

    @pl.when(step == 0)
    def _():
        load_table.start()
        if n_prev:
            new_accum_ref[...] = prev_refs[1][...]

        def zero(i, carry):
            for acc in accs:
                acc[pl.ds(pl.multiple_of(i * 64, 64), 64), :] = jnp.zeros((64, LANES), jnp.float32)
            return carry

        lax.fori_loop(0, n_rows // 64, zero, 0)

    count = count_ref[step]

    def widen(i, carry):
        rows = pl.ds(pl.multiple_of(i * LANES, LANES), LANES)
        grad_f32[rows, :] = grad_ref[rows, :].astype(jnp.float32)
        return carry

    lax.fori_loop(0, (count + LANES - 1) // LANES, widen, 0)

    def add_rows(i, carry):
        base = i * UNROLL
        for first in range(0, UNROLL, N_ACC):
            rows = [ids_ref[step * cap + base + first + k] for k in range(N_ACC)]
            sums = [accs[k][pl.ds(rows[k], 1), :] + grad_f32[pl.ds(base + first + k, 1), :] for k in range(N_ACC)]
            for k in range(N_ACC):
                accs[k][pl.ds(rows[k], 1), :] = sums[k]
        return carry

    lax.fori_loop(0, (count + UNROLL - 1) // UNROLL, add_rows, 0)

    @pl.when(step == pl.num_programs(0) - 1)
    def _():
        lr = lr_ref[0]
        diag = lax.broadcasted_iota(jnp.int32, (LANES, LANES), 0) == lax.broadcasted_iota(jnp.int32, (LANES, LANES), 1)

        def square(i, carry):
            rows = pl.ds(pl.multiple_of(i * LANES, LANES), LANES)
            grad = accs[0][rows, :]
            for acc in accs[1:]:
                grad = grad + acc[rows, :]
            accs[0][rows, :] = grad
            old = jnp.broadcast_to(accum_ref[slot : slot + 1, rows], (LANES, LANES))
            col = jnp.sum(grad * grad * (1.0 / LANES) + jnp.where(diag, old, 0.0), axis=1, keepdims=True)
            row = jnp.sum(jnp.where(diag, col, 0.0), axis=0, keepdims=True)
            new_accum_ref[slot : slot + 1, rows] = row
            scale_ref[pl.ds(i, 1), :] = row
            return carry

        lax.fori_loop(0, n_rows // LANES, square, 0)
        scale_ref[...] = lr / (jnp.sqrt(scale_ref[...]) + EPSILON)
        load_table.wait()
        part = n_rows // n_out

        def store_part(k):
            rows = pl.ds(pl.multiple_of(k * part, part), part)
            return pltpu.make_async_copy(table.at[rows, :], new_table_hbm.at[slot, rows, :], sems.at[k])

        def update_part(k, carry):
            def update(m, carry):
                i = k * (part // LANES) + m
                rows = pl.ds(pl.multiple_of(i * LANES, LANES), LANES)
                scale = jnp.sum(jnp.where(diag, jnp.broadcast_to(scale_ref[pl.ds(i, 1), :], (LANES, LANES)), 0.0), axis=1, keepdims=True)
                table[rows, :] = (table[rows, :].astype(jnp.float32) - accs[0][rows, :] * scale).astype(jnp.bfloat16)
                return carry

            lax.fori_loop(0, part // LANES, update, 0)
            store_part(k).start()
            return carry

        lax.fori_loop(0, n_out, update_part, 0)

        def finish(k, carry):
            store_part(k).wait()
            return carry

        lax.fori_loop(0, n_out, finish, 0)


def scatter_adagrad(slot, ids, counts, learn_rate, grads, tables, accum, prev):
    n_src, cap, dim = grads.shape
    n_rows = tables.shape[1]
    n_out = 8
    whole_accum = pl.BlockSpec(accum.shape, lambda s, *_: (0, 0))
    grid_spec = pltpu.PrefetchScalarGridSpec(
        num_scalar_prefetch=3,
        grid=(n_src,),
        in_specs=[
            pl.BlockSpec((None, cap, dim), lambda s, *_: (s, 0, 0)),
            pl.BlockSpec(memory_space=pl.ANY),
            whole_accum,
        ]
        + ([pl.BlockSpec(memory_space=pl.ANY), whole_accum] if prev else []),
        out_specs=[pl.BlockSpec(memory_space=pl.ANY), whole_accum],
        scratch_shapes=[
            pltpu.VMEM((cap, dim), jnp.float32),
            pltpu.VMEM((n_rows, dim), jnp.bfloat16),
            pltpu.VMEM((n_rows // LANES, LANES), jnp.float32),
            pltpu.SemaphoreType.DMA((n_out + 1,)),
        ]
        + [pltpu.VMEM((n_rows + 8, dim), jnp.float32) for _ in range(N_ACC)],
    )
    return pl.pallas_call(
        functools.partial(scatter_adagrad_kernel, slot, len(prev)),
        grid_spec=grid_spec,
        out_shape=[jax.ShapeDtypeStruct(tables.shape, tables.dtype), jax.ShapeDtypeStruct(accum.shape, accum.dtype)],
        input_output_aliases={6: 0, 7: 1} if prev else {},
        compiler_params=pltpu.CompilerParams(vmem_limit_bytes=52 * MIB),
        cost_estimate=pl.CostEstimate(flops=4_000_000_000, bytes_accessed=16 * MIB, transcendentals=0),
        name="scatter_adagrad",
    )(ids, counts, learn_rate, grads, tables, accum, *prev)


def solution(mesh):
    n_group = mesh.shape['mp']
    slot_spec = P(('pod', 'mp'))

    def packed_step(cap, by_slot, ids, own_codes, codes, tables, accum, lr):
        slots_dev, n_rows, _ = tables.shape
        per_group = codes.shape[1] - FLAG_ROWS
        blocks = per_group // slots_dev
        firsts = (codes[:, :per_group, 0] >> 1).reshape(-1)
        own_firsts = (own_codes[:, :per_group, 0] >> 1).reshape(-1)
        last = own_codes[:, blocks - 1 : per_group : blocks, LANES - 1]
        counts = ((last + 1) >> 1).T
        packed_ids = None
        recv = []
        for j in range(slots_dev):
            send = pack_rows(j, slots_dev, cap, firsts, codes, by_slot)
            if recv:
                send, recv[-1] = lax.optimization_barrier((send, recv[-1]))
            recv.append(lax.all_to_all(send, 'mp', 0, 0, tiled=True))
        packed_ids = pack_ids(cap, own_firsts, own_codes, ids, n_rows).reshape(slots_dev, -1)
        out = ()
        for j in range(slots_dev):
            out = scatter_adagrad(j, packed_ids[j], counts[j], lr, recv[j], tables, accum, out)
        return tuple(out)

    def local_step(d_pool, row_ids, lengths, tables, row_accum, learn_rate):
        batch = d_pool.shape[0]
        by_slot = jnp.swapaxes(d_pool, 0, 1)
        own_codes = bag_positions(lengths, n_group)
        codes = lax.all_to_all(own_codes, 'mp', 0, 0, tiled=True)
        largest = jnp.max(codes[:, -1, 0])
        caps = [batch * share // 16 for share in CAPACITY_SHARES]
        level = sum((largest > cap).astype(jnp.int32) for cap in caps[:-1])
        branches = [functools.partial(packed_step, cap) for cap in caps]
        return lax.switch(level, branches, by_slot, row_ids[:, :, 0], own_codes, codes, tables, row_accum, learn_rate.reshape(1))

    return jax.shard_map(local_step, mesh=mesh, in_specs=(slot_spec, slot_spec, slot_spec, slot_spec, slot_spec, P()), out_specs=(slot_spec, slot_spec), check_vma=False)
```

time: 406 us -> 346 us (0.85)
  the two profiles are of different devices: /device:TPU:119 before, /device:TPU:112 now
where the time goes in v2:
time: 346 us; the launch traced here: 344 us
  Pallas kernels  236 us (68%)
  waiting for transfers between devices  65.8 us (19%)
  starting transfers between devices  16 us (5%)
  blocking collectives  13 us (4%)
  local copies, waits for them, and re-layouts  9.8 us (3%)
    pallas_call x4, Pallas kernels, scatter_adagrad(): pl.pallas_call(functools.partial(scatter_adagrad_kernel, slot, len(prev))...  189 us
    all_to_all x4, waiting for transfers between devices, packed_step(): recv.append(lax.all_to_all(send, 'mp', 0, 0, tiled=True))  65.8 us
    pallas_call x4, Pallas kernels, pack_rows(): pl.pallas_call(functools.partial(pack_rows_kernel, slot, n_tab, slots_dev...  30.5 us
    all_to_all x4, starting transfers between devices, packed_step(): recv.append(lax.all_to_all(send, 'mp', 0, 0, tiled=True))  16 us
    pallas_call x1, Pallas kernels, pack_ids(): pl.pallas_call(functools.partial(pack_ids_kernel, n_rows=n_rows), grid_sp...  15.4 us
    all_to_all x1, blocking collectives, local_step(): codes = lax.all_to_all(own_codes, 'mp', 0, 0, tiled=True)  13 us
  transfers between devices with their start and end apart: 4, of which 3 were waited for; matrix products, arithmetic and copies ran while one was open for 1% of the time, Pallas kernels for 52%

profile of v2, /device:TPU:112, one launch (start us, length us, event | category | flops | bytes accessed | tf_op | source)
XLA Modules:
  0.0 344.1 jit_solution(2376766373313441905)
XLA Ops:
  0.6 1.8 reshape.73.lens_ref
  2.5 1.5 bag_positions.1
  3.9 13.0 %all_to_all.53 = s32[8,72,128]{2,1,0:T(8,128)S(1)} all-to-all(s32[8,72,128]{2,1,0:T(8,128)S(1)} %bag_positions.1), channel_id=1, replica_groups=mesh['pod'=2,'mp'=8] {'mp'}, dimensions={0} | all-to-all | bytes 589824 | tf_op jit(solution)/shard_map/all_to_all | solution.py:309
  16.9 0.6 slice_reduce_fusion
  18.8 325.1 %conditional.1 = ((bf16[4,16384,128]{2,1,0:T(8,128)(2,1)}, f32[4,16384]{1,0:T(4,128)})) conditional(s32[]{:T(128)} %clamp.3, (s32[8,72,128]{2,1,0:T(8,128)S(1)}, s32[4,16384,1]{1,2,0:T(1,128)}, s32[8,72,128]{2,1,0:T(8,128)S(1)}, bf16[26,2048,128]{2,1,0:T(8,128)(2,1)}, f32[]{:T(128)}, /*index=5*/bf16[4,16384,128]{2,1,0:T(8,128)(2,1)}, ...), branch_computations={%region_1.0_spmd, %region_2.0_spmd, %region_3.0_spmd} | conditional | flops 19000000512 | bytes 161924128 | solution.py:314
  18.8 0.2 shift-right-arithmetic_reduce_fusion
  19.0 0.7 shift_right_arithmetic.47.first_ref
  19.7 7.9 %pack_rows.15 = bf16[8,1152,128]{2,1,0:T(8,128)(2,1)} custom-call(s32[512]{0:T(512)} %shift_right_arithmetic.47.first_ref, s32[8,72,128]{2,1,0:T(8,128)S(1)} %get-tuple-element.45.code_ref, bf16[26,2048,128]{2,1,0:T(8,128)(2,1)} %get-tuple-element.46.grad_ref), custom_call_target="tpu_custom_call" | custom-call | flops 500000000 | bytes 8388608 | tf_op jit(solution)/shard_map/cond/branch_0_fun/pack_rows/pallas_call | solution.py:94
  27.6 3.8 %all-to-all-start = ((bf16[8,1152,128]{2,1,0:T(8,128)(2,1)}), bf16[8,1152,128]{2,1,0:T(8,128)(2,1)S(1)}, u32[]{:S(2)}, u32[]{:S(2)}) async-start(bf16[8,1152,128]{2,1,0:T(8,128)(2,1)} %pack_rows.15), calls=%async_computation | async-start | bytes 4718592 | tf_op jit(solution)/shard_map/cond/branch_0_fun/all_to_all | solution.py:298
  31.4 7.8 %pack_rows.14 = bf16[8,1152,128]{2,1,0:T(8,128)(2,1)} custom-call(s32[512]{0:T(512)} %shift_right_arithmetic.47.first_ref, s32[8,72,128]{2,1,0:T(8,128)S(1)} %get-tuple-element.45.code_ref, bf16[26,2048,128]{2,1,0:T(8,128)(2,1)} %get-tuple-element.46.grad_ref), custom_call_target="tpu_custom_call" | custom-call | flops 500000000 | bytes 8388608 | tf_op jit(solution)/shard_map/cond/branch_0_fun/pack_rows/pallas_call | solution.py:94
  39.2 22.0 %all-to-all-done.grad_ref = bf16[8,1152,128]{2,1,0:T(8,128)(2,1)S(1)} async-done(((bf16[8,1152,128]{2,1,0:T(8,128)(2,1)}), bf16[8,1152,128]{2,1,0:T(8,128)(2,1)S(1)}, u32[]{:S(2)}, u32[]{:S(2)}) %all-to-all-start) | async-done | bytes 2359328 | tf_op jit(solution)/shard_map/cond/branch_0_fun/all_to_all | solution.py:298
  61.2 0.0 copy-start.5
  61.2 1.4 copy-done.5
  62.6 3.8 %all-to-all-start.1 = ((bf16[8,1152,128]{2,1,0:T(8,128)(2,1)}), bf16[8,1152,128]{2,1,0:T(8,128)(2,1)S(1)}, u32[]{:S(2)}, u32[]{:S(2)}) async-start(bf16[8,1152,128]{2,1,0:T(8,128)(2,1)} %pack_rows.14), calls=%async_computation.1 | async-start | bytes 4718592 | tf_op jit(solution)/shard_map/cond/branch_0_fun/all_to_all | solution.py:298
  66.4 7.4 %pack_rows.13 = bf16[8,1152,128]{2,1,0:T(8,128)(2,1)} custom-call(s32[512]{0:T(512)} %shift_right_arithmetic.47.first_ref, s32[8,72,128]{2,1,0:T(8,128)S(1)} %get-tuple-element.45.code_ref, bf16[26,2048,128]{2,1,0:T(8,128)(2,1)} %get-tuple-element.46.grad_ref), custom_call_target="tpu_custom_call" | custom-call | flops 500000000 | bytes 8388608 | tf_op jit(solution)/shard_map/cond/branch_0_fun/pack_rows/pallas_call | solution.py:94
  73.8 22.4 %all-to-all-done.1.grad_ref = bf16[8,1152,128]{2,1,0:T(8,128)(2,1)S(1)} async-done(((bf16[8,1152,128]{2,1,0:T(8,128)(2,1)}), bf16[8,1152,128]{2,1,0:T(8,128)(2,1)S(1)}, u32[]{:S(2)}, u32[]{:S(2)}) %all-to-all-start.1) | async-done | bytes 2359328 | tf_op jit(solution)/shard_map/cond/branch_0_fun/all_to_all | solution.py:298
  96.2 0.0 copy-start.3
  96.2 4.6 %all-to-all-start.2 = ((bf16[8,1152,128]{2,1,0:T(8,128)(2,1)}), bf16[8,1152,128]{2,1,0:T(8,128)(2,1)}, u32[]{:S(2)}, u32[]{:S(2)}) async-start(bf16[8,1152,128]{2,1,0:T(8,128)(2,1)} %pack_rows.13), calls=%async_computation.2 | async-start | bytes 4718592 | tf_op jit(solution)/shard_map/cond/branch_0_fun/all_to_all | solution.py:298
  100.8 0.2 shift-right-arithmetic_reduce_fusion.1
  101.0 0.7 shift_right_arithmetic.43.first_ref
  101.6 7.4 %pack_rows.12 = bf16[8,1152,128]{2,1,0:T(8,128)(2,1)} custom-call(s32[512]{0:T(512)} %shift_right_arithmetic.47.first_ref, s32[8,72,128]{2,1,0:T(8,128)S(1)} %get-tuple-element.45.code_ref, bf16[26,2048,128]{2,1,0:T(8,128)(2,1)} %get-tuple-element.46.grad_ref), custom_call_target="tpu_custom_call" | custom-call | flops 500000000 | bytes 8388608 | tf_op jit(solution)/shard_map/cond/branch_0_fun/pack_rows/pallas_call | solution.py:94
  109.1 0.0 copy-done.3
  109.1 0.0 copy-start.7
  109.1 21.5 %all-to-all-done.2.grad_ref = bf16[8,1152,128]{2,1,0:T(8,128)(2,1)} async-done(((bf16[8,1152,128]{2,1,0:T(8,128)(2,1)}), bf16[8,1152,128]{2,1,0:T(8,128)(2,1)}, u32[]{:S(2)}, u32[]{:S(2)}) %all-to-all-start.2) | async-done | bytes 2359328 | tf_op jit(solution)/shard_map/cond/branch_0_fun/all_to_all | solution.py:298
  130.6 3.8 %all-to-all-start.3 = ((bf16[8,1152,128]{2,1,0:T(8,128)(2,1)}), bf16[8,1152,128]{2,1,0:T(8,128)(2,1)S(1)}, u32[]{:S(2)}, u32[]{:S(2)}) async-start(bf16[8,1152,128]{2,1,0:T(8,128)(2,1)} %pack_rows.12), calls=%async_computation.3 | async-start | bytes 4718592 | tf_op jit(solution)/shard_map/cond/branch_0_fun/all_to_all | solution.py:298
  134.4 0.0 copy-done.7
  134.5 0.0 copy-start
  134.5 15.4 %pack_ids.3 = s32[4,72,128]{2,1,0:T(8,128)} custom-call(s32[512]{0:T(512)} %shift_right_arithmetic.43.first_ref, s32[8,72,128]{2,1,0:T(8,128)S(1)} %get-tuple-element.42.code_ref, s32[4,128,128]{2,1,0:T(8,128)S(1)} %bitcast.70), custom_call_target="tpu_custom_call" | custom-call | flops 1000000000 | bytes 1048576 | tf_op jit(solution)/shard_map/cond/branch_0_fun/pack_ids/pallas_call | solution.py:147
  149.9 0.0 copy-start.6
  149.9 3.0 copy.56
  152.9 0.8 slice.82
  153.7 0.0 copy-done.6
  153.7 0.0 copy-done
  153.7 47.0 %scatter_adagrad.12 = (bf16[4,16384,128]{2,1,0:T(8,128)(2,1)}, f32[4,16384]{1,0:T(4,128)}) custom-call(s32[9216]{0:T(1024)S(1)} %get-tuple-element.199.ids_ref, s32[8]{0:T(128)S(1)} %get-tuple-element.203.count_ref, f32[1]{0:T(128)} %bitcast.5.lr_ref, bf16[8,1152,128]{2,1,0:T(8,128)(2,1)} %copy-done.5, bf16[4,16384,128]{2,1,0:T(8,128)(2,1)} %get-tuple-element.127.table_hbm, ...), custom_call_target="tpu_custom_call" | custom-call | flops 4000000000 | bytes 16777216 | tf_op jit(solution)/shard_map/cond/branch_0_fun/scatter_adagrad/pallas_call | solution.py:269
  200.7 47.2 %scatter_adagrad.13 = (bf16[4,16384,128]{2,1,0:T(8,128)(2,1)}, f32[4,16384]{1,0:T(4,128)}) custom-call(s32[9216]{0:T(1024)S(1)} %get-tuple-element.200.ids_ref, s32[8]{0:T(128)S(1)} %get-tuple-element.204.count_ref, f32[1]{0:T(128)} %bitcast.5.lr_ref, bf16[8,1152,128]{2,1,0:T(8,128)(2,1)} %copy-done.3, ...), custom_call_target="tpu_custom_call", output_to_operand_aliasing={{0}: (6, {}), {1}: (7, {})} | custom-call | flops 4000000000 | bytes 16777216 | tf_op jit(solution)/shard_map/cond/branch_0_fun/scatter_adagrad/pallas_call | solution.py:269
  247.8 47.2 %scatter_adagrad.14 = (bf16[4,16384,128]{2,1,0:T(8,128)(2,1)}, f32[4,16384]{1,0:T(4,128)}) custom-call(s32[9216]{0:T(1024)S(1)} %get-tuple-element.201.ids_ref, s32[8]{0:T(128)S(1)} %get-tuple-element.205.count_ref, f32[1]{0:T(128)} %bitcast.5.lr_ref, bf16[8,1152,128]{2,1,0:T(8,128)(2,1)} %all-to-all-done.2.grad_ref, ...), custom_call_target="tpu_custom_call", output_to_operand_aliasing={{0}: (6, {}), {1}: (7, {})} | custom-call | flops 4000000000 | bytes 16777216 | tf_op jit(solution)/shard_map/cond/branch_0_fun/scatter_adagrad/pallas_call | solution.py:269
  295.1 0.0 all-to-all-done.3.grad_ref
  295.1 0.0 copy-start.4
  295.1 1.4 copy-done.4
  296.5 47.2 %scatter_adagrad.15 = (bf16[4,16384,128]{2,1,0:T(8,128)(2,1)}, f32[4,16384]{1,0:T(4,128)}) custom-call(s32[9216]{0:T(1024)S(1)} %get-tuple-element.202.ids_ref, s32[8]{0:T(128)S(1)} %get-tuple-element.206.count_ref, f32[1]{0:T(128)} %bitcast.5.lr_ref, bf16[8,1152,128]{2,1,0:T(8,128)(2,1)} %copy-done.4, ...), custom_call_target="tpu_custom_call", output_to_operand_aliasing={{0}: (6, {}), {1}: (7, {})} | custom-call | flops 4000000000 | bytes 16777216 | tf_op jit(solution)/shard_map/cond/branch_0_fun/scatter_adagrad/pallas_call | solution.py:269
  (3 shorter events, 0.0 us)
Async XLA Ops:
  27.6 33.6 %all-to-all-start = ((bf16[8,1152,128]{2,1,0:T(8,128)(2,1)}), bf16[8,1152,128]{2,1,0:T(8,128)(2,1)S(1)}, u32[]{:S(2)}, u32[]{:S(2)}) async-start(bf16[8,1152,128]{2,1,0:T(8,128)(2,1)} %pack_rows.15), calls=%async_computation | async-start | bytes 4718592 | tf_op jit(solution)/shard_map/cond/branch_0_fun/all_to_all | solution.py:298
  61.2 1.4 copy-start.5
  62.6 33.6 %all-to-all-start.1 = ((bf16[8,1152,128]{2,1,0:T(8,128)(2,1)}), bf16[8,1152,128]{2,1,0:T(8,128)(2,1)S(1)}, u32[]{:S(2)}, u32[]{:S(2)}) async-start(bf16[8,1152,128]{2,1,0:T(8,128)(2,1)} %pack_rows.14), calls=%async_computation.1 | async-start | bytes 4718592 | tf_op jit(solution)/shard_map/cond/branch_0_fun/all_to_all | solution.py:298
  96.2 12.9 %copy-start.3 = (bf16[8,1152,128]{2,1,0:T(8,128)(2,1)}, bf16[8,1152,128]{2,1,0:T(8,128)(2,1)S(1)}, u32[]{:S(2)}) copy-start(bf16[8,1152,128]{2,1,0:T(8,128)(2,1)S(1)} %all-to-all-done.1.grad_ref) | copy-start | bytes 7077892 | tf_op jit(solution)/shard_map/cond
  96.2 34.4 %all-to-all-start.2 = ((bf16[8,1152,128]{2,1,0:T(8,128)(2,1)}), bf16[8,1152,128]{2,1,0:T(8,128)(2,1)}, u32[]{:S(2)}, u32[]{:S(2)}) async-start(bf16[8,1152,128]{2,1,0:T(8,128)(2,1)} %pack_rows.13), calls=%async_computation.2 | async-start | bytes 4718592 | tf_op jit(solution)/shard_map/cond/branch_0_fun/all_to_all | solution.py:298
  109.1 25.4 %copy-start.7 = (s32[4,16384,1]{1,2,0:T(1,128)S(1)}, s32[4,16384,1]{1,2,0:T(1,128)}, u32[]{:S(2)}) copy-start(s32[4,16384,1]{1,2,0:T(1,128)} %get-tuple-element.179) | copy-start | bytes 786436 | tf_op jit(solution)/shard_map/cond
  130.6 164.5 %all-to-all-start.3 = ((bf16[8,1152,128]{2,1,0:T(8,128)(2,1)}), bf16[8,1152,128]{2,1,0:T(8,128)(2,1)S(1)}, u32[]{:S(2)}, u32[]{:S(2)}) async-start(bf16[8,1152,128]{2,1,0:T(8,128)(2,1)} %pack_rows.12), calls=%async_computation.3 | async-start | bytes 4718592 | tf_op jit(solution)/shard_map/cond/branch_0_fun/all_to_all | solution.py:298
  134.5 19.2 %copy-start = (f32[4,16384]{1,0:T(4,128)S(1)}, f32[4,16384]{1,0:T(4,128)}, u32[]{:S(2)}) copy-start(f32[4,16384]{1,0:T(4,128)} %get-tuple-element.130.accum_ref) | copy-start | bytes 786436 | tf_op jit(solution)/shard_map/cond
  149.9 3.8 %copy-start.6 = (s32[4,72,128]{2,1,0:T(8,128)S(1)}, s32[4,72,128]{2,1,0:T(8,128)}, u32[]{:S(2)}) copy-start(s32[4,72,128]{2,1,0:T(8,128)} %pack_ids.3) | copy-start | bytes 442372 | tf_op jit(solution)/shard_map/cond
  295.1 1.4 copy-start.4
